TPU v7x, 32 devices: a whole 2x2x4 slice. The times are simulated.
32 devices in a mesh: doc: 4 (over y, x), ctx: 8 (over z, core).
Axes of the slice: x: 2, y: 2, z: 4, core: 2. Of those that a mesh axis runs over, the one named last changes fastest.
Arguments:
- summary_cache: bfloat16 [8, 16, 512, 2048], P(None, 'doc', None, 'ctx'), may hold values from -4 to 4
- queries: bfloat16 [4, 2048, 4096], P('doc', 'ctx'), may hold values from -100 to 100
- section_counts: int32 [16], replicated, may hold values from 1 to 2
- summary_blocks: int32 [16, 2], replicated, may hold values from 1 to 2
Outputs:
- attended: bfloat16 [4, 2048, 4096], P('doc', 'ctx')
- relayed: bfloat16 [8, 4, 2048, 2048], P(None, 'doc', 'ctx')
All inputs are finite; a program needn't handle non-finite values.
Results may differ from a plain program's by a relative error of at most 0.0045.
Values may be sent and summed in bfloat16 or wider, within the bound.
A program may use at most 192 MiB of HBM per device.

v0:
```python
import math

import jax
import jax.numpy as jnp
from jax import lax
from jax.sharding import PartitionSpec as P

QH = 32
KVH = 8
HD = 128
BLOCK = 128
SECTIONS = 2
GROUP = 4
SUMLEN = 256


NEGATIVE = -1e30


def relay(cache_part):
    layers, documents, slot_count, feature_count = cache_part.shape
    flattened = cache_part.reshape(layers, documents * slot_count, feature_count)
    return lax.all_to_all(
        lax.all_to_all(flattened, "doc", split_axis=1, concat_axis=1, tiled=True),
        "ctx",
        split_axis=1,
        concat_axis=2,
        tiled=True,
    )


def group_validity(section_counts, summary_blocks, group_index, row_count):
    chosen = (jnp.arange(row_count) == group_index).astype(jnp.int32)
    counts_all = section_counts.reshape(row_count, row_count)
    blocks_all = summary_blocks.reshape(row_count, row_count, SECTIONS)
    counts_here = jnp.sum(counts_all * chosen[None, :], axis=1)
    blocks_here = jnp.sum(blocks_all * chosen[None, :, None], axis=1)
    live_section = jnp.arange(SECTIONS)[None, :] < counts_here[:, None]
    live_slot = jnp.arange(SUMLEN)[None, None, :] < BLOCK * blocks_here[:, :, None]
    return (live_section[:, :, None] & live_slot).reshape(row_count * SECTIONS * SUMLEN)


def attend(attn_state, key_piece, first_row, grouped_queries, query_positions, validity):
    piece_rows = key_piece.shape[0]
    block_rows = math.gcd(piece_rows, 512)
    own_last = query_positions[-1]

    def compute(state_now):
        running_max, denominator, accumulated = state_now
        key_heads = key_piece[:, : KVH * HD].reshape(block_rows, KVH, HD)
        value_heads = key_piece[:, KVH * HD :].reshape(block_rows, KVH, HD)
        scores = jnp.einsum(
            "pkgd,skd->kgps", grouped_queries, key_heads, preferred_element_type=jnp.float32
        ) * (1.0 / math.sqrt(HD))
        key_positions = first_row + jnp.arange(block_rows)
        live_keys = lax.dynamic_slice_in_dim(validity, first_row, block_rows)
        allowed = live_keys[None, :] & (key_positions[None, :] <= query_positions[:, None])
        masked = jnp.where(allowed, scores, NEGATIVE)
        newest = jnp.maximum(running_max, jnp.max(masked, axis=-1))
        weights = jnp.where(allowed, jnp.exp(masked - newest[..., None]), 0.0)
        factor = jnp.exp(running_max - newest)
        denominator = denominator * factor + jnp.sum(weights, axis=-1)
        accumulated = accumulated * factor[..., None] + jnp.einsum(
            "kgps,skd->kgpd",
            weights.astype(jnp.bfloat16),
            value_heads,
            preferred_element_type=jnp.float32,
        )
        return (newest, denominator, accumulated)

    return lax.cond(
        first_row <= own_last, compute, lambda unchanged_state: unchanged_state, attn_state
    )


def finish(attn_state, own_rows):
    running_max, denominator, accumulated = attn_state
    result = accumulated / denominator[..., None]
    return jnp.transpose(result, (2, 0, 1, 3)).reshape(1, own_rows, QH * HD).astype(jnp.bfloat16)


def local(summary_cache, queries, section_counts, summary_blocks):
    row_count = lax.axis_size("doc")
    group_index = lax.axis_index("doc")
    shard_index = lax.axis_index("ctx")
    own_rows = queries.shape[1]
    validity = group_validity(section_counts, summary_blocks, group_index, row_count)
    query_positions = shard_index * own_rows + jnp.arange(own_rows)
    grouped_queries = queries[0].reshape(own_rows, KVH, GROUP, HD)
    initial = (
        jnp.full((KVH, GROUP, own_rows), NEGATIVE, jnp.float32),
        jnp.zeros((KVH, GROUP, own_rows), jnp.float32),
        jnp.zeros((KVH, GROUP, own_rows, HD), jnp.float32),
    )
    layers, documents, slot_count, feature_count = summary_cache.shape
    grouped = lax.all_to_all(
        summary_cache[0].reshape(documents * slot_count, feature_count),
        "doc",
        split_axis=0,
        concat_axis=0,
        tiled=True,
    )
    whole_group = lax.all_gather(grouped, "ctx", axis=1, tiled=True)
    group_rows = whole_group.shape[0]
    block_span = math.gcd(group_rows, 512)
    attn_state = initial
    for offset in range(0, group_rows, block_span):
        attn_state = attend(
            attn_state,
            whole_group[offset : offset + block_span],
            offset,
            grouped_queries,
            query_positions,
            validity,
        )
    own_first = lax.dynamic_slice_in_dim(whole_group, shard_index * own_rows, own_rows, 0)
    relayed_local = jnp.concatenate([own_first[None], relay(summary_cache[1:])], axis=0)
    attended = finish(attn_state, own_rows)
    return (
        attended,
        relayed_local.reshape(relayed_local.shape[0], 1, own_rows, relayed_local.shape[2]),
    )


def solution(mesh):
    placed = (P(None, "doc", None, "ctx"), P("doc", "ctx", None), P(), P())
    return jax.shard_map(
        local,
        mesh=mesh,
        in_specs=placed,
        out_specs=(P("doc", "ctx", None), P(None, "doc", "ctx", None)),
        check_vma=False,
    )
```

profile of v0, /device:TPU:13, one launch (start us, length us, event | category | flops | bytes accessed | tf_op | source)
XLA Modules:
  0.0 348.4 jit_solution(13529874175803715797)
XLA Ops:
  7.2 2.3 slice_bitcast_fusion
  9.4 4.5 %all-to-all-start = ((bf16[4,512,256]{2,1,0:T(8,128)(2,1)}), bf16[4,512,256]{2,1,0:T(8,128)(2,1)}, u32[]{:S(2)}, u32[]{:S(2)}) async-start(bf16[4,512,256]{2,1,0:T(8,128)(2,1)} %slice_bitcast_fusion), calls=%async_computation | async-start | bytes 2097152 | tf_op jit(solution)/shard_map/all_to_all | solution.py:96
  13.9 0.0 slice-start
  13.9 3.1 slice-done
  17.0 7.9 %copy.72 = bf16[7,4,512,256]{3,0,2,1:T(8,128)(2,1)} copy(bf16[7,4,512,256]{3,2,1,0:T(8,128)(2,1)S(1)} %slice-done) | data formatting | bytes 14680064 | tf_op jit(solution)/shard_map/slice | solution.py:117
  24.9 2.0 all-to-all-done
  26.8 0.0 copy-start.2
  26.8 0.0 copy-start.3
  26.8 6.1 %all-to-all-start.1 = ((bf16[7,2048,256]{2,0,1:T(8,128)(2,1)}), bf16[7,2048,256]{2,0,1:T(8,128)(2,1)}, u32[]{:S(2)}, u32[]{:S(2)}) async-start(bf16[7,2048,256]{2,0,1:T(8,128)(2,1)} %bitcast.147), calls=%async_computation.1 | async-start | bytes 16777216 | tf_op jit(solution)/shard_map/all_to_all | solution.py:24
  32.9 0.0 all-gather.2.cloned.1.call-start
  32.9 2.3 copy.108
  35.2 0.0 all-gather.2.cloned.1.call-update
  35.2 88.5 %all-to-all-done.1 = bf16[7,2048,256]{2,0,1:T(8,128)(2,1)} async-done(((bf16[7,2048,256]{2,0,1:T(8,128)(2,1)}), bf16[7,2048,256]{2,0,1:T(8,128)(2,1)}, u32[]{:S(2)}, u32[]{:S(2)}) %all-to-all-start.1) | async-done | bytes 7340064 | tf_op jit(solution)/shard_map/all_to_all | solution.py:24
  123.7 7.2 %all-to-all-start.2 = ((bf16[7,2048,256]{2,0,1:T(8,128)(2,1)}), bf16[7,2048,256]{2,0,1:T(8,128)(2,1)}, u32[]{:S(2)}, u32[]{:S(2)}) async-start(bf16[7,2048,256]{2,0,1:T(8,128)(2,1)} %all-to-all-done.1), calls=%async_computation.2 | async-start | bytes 16777216 | tf_op jit(solution)/shard_map/all_to_all | solution.py:23
  130.9 0.0 copy-done.2
  130.9 0.1 reshape.149
  131.0 0.1 multiply_reduce_fusion
  131.1 0.1 copy.64
  131.2 0.0 copy-done.3
  131.2 0.1 reshape.148
  131.3 0.1 multiply_reduce_fusion.1
  131.4 0.1 iota_compare_fusion.1
  131.5 0.1 compare_and_fusion.3
  131.6 3.3 copy.66
  134.9 0.0 copy-start
  134.9 0.7 slice.50
  138.2 0.0 all-gather.2.cloned.1.call-done
  138.2 3.8 %fusion.51 = (bf16[512,2048]{0,1:T(8,128)(2,1)}, bf16[512,2048]{0,1:T(8,128)(2,1)S(1)}) fusion(bf16[2048,2048]{0,1:T(8,128)(2,1)} %all-gather.2.cloned.1.call-done), kind=kLoop, calls=%fused_computation.77 | loop fusion | bytes 8388608 | tf_op jit(solution)/shard_map/slice | solution.py:110
  142.1 17.4 %conditional.4 = (f32[8,4,256]{2,1,0:T(4,128)}, f32[8,4,256]{2,1,0:T(4,128)S(1)}, f32[8,4,256,128]{3,2,1,0:T(8,128)}) conditional(s32[]{:T(128)} %bitcast.23, () %tuple.35, (pred[2048]{0:T(1024)(128)(4,1)S(1)}, s32[256]{0:T(256)S(1)}, bf16[512,2048]{0,1:T(8,128)(2,1)S(1)}, bf16[256,8,4,128]{0,3,2,1:T(8,128)(2,1)S(1)}) %tuple.88), branch_computations={%region_2.0_spmd, %region_3.6_spmd} | conditional | flops 2203353088 | bytes 63801880 | solution.py:71
  142.1 0.1 fusion.8
  142.2 0.1 fusion.47
  142.4 2.8 fusion
  145.1 0.6 exponential_multiply_fusion
  145.7 5.1 %fusion.2 = f32[8,4,256]{2,1,0:T(4,128)S(1)} fusion(f32[8,512,256,4]{2,1,3,0:T(8,128)S(1)} %get-tuple-element.207, f32[8,4,256]{2,1,0:T(4,128)} %get-tuple-element.231, pred[256,512]{0,1:T(8,128)(4,1)S(1)} %fusion.8), kind=kLoop, calls=%fused_computation.4 | loop fusion | flops 20963328 | bytes 16973824 | tf_op jit(solution)/shard_map/cond/branch_1_fun/reduce_sum | solution.py:62
  150.8 0.8 fusion.12
  151.6 7.9 %broadcast_add_fusion = f32[8,4,256,128]{3,2,1,0:T(8,128)} fusion(f32[8,4,256]{2,1,0:T(4,128)S(1)} %get-tuple-element.196, bf16[512,8,128,1]{0,2,3,1:T(8,128)(2,1)S(1)} %bitcast.156, f32[8,512,256,4]{2,1,3,0:T(8,128)S(1)} %get-tuple-element.207, f32[8,4,256]{2,1,0:T(4,128)} %get-tuple-element.231, pred[256,512]{0,1:T(8,128)(4,1)S(1)} %fusion.8), kind=kOutput, calls=%fused_computation.7 | convolution fusion | flops 1095761920 | bytes 22216704 | tf_op jit(solution)/shard_map/cond/branch_1_fun/kgps,skd->kgpd/dot_general | solution.py:63
  159.5 0.0 copy-done
  159.5 23.1 %conditional.5 = ((f32[8,4,256]{2,1,0:T(4,128)}, f32[8,4,256]{2,1,0:T(4,128)S(1)}, f32[8,4,256,128]{3,2,1,0:T(8,128)})) conditional(s32[]{:T(128)} %bitcast.22, (f32[8,4,256]{2,1,0:T(4,128)}, f32[8,4,256]{2,1,0:T(4,128)S(1)}, f32[8,4,256,128]{3,2,1,0:T(8,128)}) %conditional.4, (pred[2048]{0:T(1024)(128)(4,1)S(1)}, s32[256]{0:T(256)S(1)}, ...), branch_computations={%region_6.7_spmd, %region_7.10_spmd} | conditional | flops 2204385792 | bytes 76552768 | solution.py:71
  159.5 0.0 copy-start.1
  159.5 0.2 compare_and_fusion
  159.8 3.2 fusion.48
  163.0 0.0 copy-done.1
  163.0 4.3 %fusion.13 = (f32[8,4,256]{2,1,0:T(4,128)S(1)}, f32[8,512,256,4]{2,1,3,0:T(8,128)S(1)}) fusion(pred[256,512]{0,1:T(8,128)(4,1)S(1)} %compare_and_fusion, bf16[512,8,128,1]{0,2,3,1:T(8,128)(2,1)S(1)} %bitcast.150, bf16[256,8,4,128]{0,3,2,1:T(8,128)(2,1)} %copy-done.1), kind=kOutput, calls=%fused_computation.18 | convolution fusion | flops 1086316544 | bytes 20086784 | tf_op jit(solution)/shard_map/cond/branch_1_fun/pkgd,skd->kgps/dot_general | solution.py:52
  167.3 0.8 max.6
  168.0 4.3 %fusion.15 = f32[8,4,256]{2,1,0:T(4,128)S(1)} fusion(f32[8,512,256,4]{2,1,3,0:T(8,128)S(1)} %get-tuple-element.211, f32[8,4,256]{2,1,0:T(4,128)S(1)} %max.6, pred[256,512]{0,1:T(8,128)(4,1)S(1)} %compare_and_fusion), kind=kLoop, calls=%fused_computation.20 | loop fusion | flops 20963328 | bytes 16973824 | tf_op jit(solution)/shard_map/cond/branch_1_fun/reduce_sum | solution.py:62
  172.3 0.8 multiply_add_fusion.1
  173.1 8.9 %multiply_add_fusion = f32[8,4,256,128]{3,2,1,0:T(8,128)} fusion(f32[8,4,256,128]{3,2,1,0:T(8,128)} %get-tuple-element.78, f32[8,4,256]{2,1,0:T(4,128)S(1)} %bitcast.170, bf16[512,8,128,1]{0,2,3,1:T(8,128)(2,1)} %bitcast.153, f32[8,512,256,4]{2,1,3,0:T(8,128)S(1)} %get-tuple-element.211, f32[8,4,256]{2,1,0:T(4,128)S(1)} %max.6, ...), kind=kOutput, calls=%fused_computation.23 | convolution fusion | flops 1096810496 | bytes 26411008 | tf_op jit(solution)/shard_map/cond/branch_1_fun/kgps,skd->kgpd/dot_general | solution.py:63
  182.0 0.6 copy.119
  182.6 2.9 fusion.46
  185.5 1.6 copy.71
  187.1 2.8 convert_element_type.75
  189.9 1.3 dynamic-slice_bitcast_fusion
  191.2 120.1 %all-to-all-done.2 = bf16[7,2048,256]{2,0,1:T(8,128)(2,1)} async-done(((bf16[7,2048,256]{2,0,1:T(8,128)(2,1)}), bf16[7,2048,256]{2,0,1:T(8,128)(2,1)}, u32[]{:S(2)}, u32[]{:S(2)}) %all-to-all-start.2) | async-done | bytes 7340064 | tf_op jit(solution)/shard_map/all_to_all | solution.py:23
  311.2 11.9 %copy.74 = bf16[7,256,8,256]{1,3,2,0:T(8,128)(2,1)} copy(bf16[7,256,8,256]{3,0,1,2:T(8,128)(2,1)} %bitcast.32) | data formatting | bytes 14680064 | tf_op jit(solution)/shard_map/all_to_all | solution.py:23
  323.2 7.0 %maximum_bitcast_fusion = bf16[8,1,256,2048]{2,3,0,1:T(8,128)(2,1)} fusion(bf16[7,256,2048]{1,2,0:T(8,128)(2,1)} %bitcast.148, bf16[1,256,2048]{1,2,0:T(8,128)(2,1)S(1)} %dynamic-slice_bitcast_fusion), kind=kLoop, calls=%fused_computation.61 | loop fusion | flops 4194304 | bytes 16777216 | tf_op jit(solution)/shard_map/reshape | solution.py:121
  330.2 11.4 %copy.75 = bf16[8,1,256,2048]{3,2,1,0:T(8,128)(2,1)} copy(bf16[8,1,256,2048]{2,3,0,1:T(8,128)(2,1)} %maximum_bitcast_fusion) | data formatting | bytes 16777216
  (9 shorter events, 0.0 us)
Async XLA Ops:
  9.4 17.4 %all-to-all-start = ((bf16[4,512,256]{2,1,0:T(8,128)(2,1)}), bf16[4,512,256]{2,1,0:T(8,128)(2,1)}, u32[]{:S(2)}, u32[]{:S(2)}) async-start(bf16[4,512,256]{2,1,0:T(8,128)(2,1)} %slice_bitcast_fusion), calls=%async_computation | async-start | bytes 2097152 | tf_op jit(solution)/shard_map/all_to_all | solution.py:96
  13.9 3.1 slice-start
  26.8 104.1 %copy-start.2 = (s32[16,2]{0,1:T(2,128)S(1)}, s32[16,2]{0,1:T(2,128)}, u32[]{:S(2)}) copy-start(s32[16,2]{0,1:T(2,128)} %param.15) | copy-start | bytes 388
  26.8 104.4 %copy-start.3 = (s32[16]{0:T(128)S(1)}, s32[16]{0:T(128)}, u32[]{:S(2)}) copy-start(s32[16]{0:T(128)} %param.14) | copy-start | bytes 196
  26.8 96.9 %all-to-all-start.1 = ((bf16[7,2048,256]{2,0,1:T(8,128)(2,1)}), bf16[7,2048,256]{2,0,1:T(8,128)(2,1)}, u32[]{:S(2)}, u32[]{:S(2)}) async-start(bf16[7,2048,256]{2,0,1:T(8,128)(2,1)} %bitcast.147), calls=%async_computation.1 | async-start | bytes 16777216 | tf_op jit(solution)/shard_map/all_to_all | solution.py:24
  32.9 105.3 %all-gather.2.cloned.1.call-start = ((), (), s32[]{:S(2)}) async-start(), calls=%async_computation.3 | async-start | bytes 9437184 | tf_op jit(solution)/shard_map/all_gather | solution.py:103
  123.7 187.5 %all-to-all-start.2 = ((bf16[7,2048,256]{2,0,1:T(8,128)(2,1)}), bf16[7,2048,256]{2,0,1:T(8,128)(2,1)}, u32[]{:S(2)}, u32[]{:S(2)}) async-start(bf16[7,2048,256]{2,0,1:T(8,128)(2,1)} %all-to-all-done.1), calls=%async_computation.2 | async-start | bytes 16777216 | tf_op jit(solution)/shard_map/all_to_all | solution.py:23
  134.9 24.6 %copy-start = (bf16[1,256,4096]{1,2,0:T(8,128)(2,1)}, bf16[1,256,4096]{1,2,0:T(8,128)(2,1)S(1)}, u32[]{:S(2)}) copy-start(bf16[1,256,4096]{1,2,0:T(8,128)(2,1)S(1)} %copy.66) | copy-start | bytes 6291460
  159.5 3.5 copy-start.1
Sparse Core Ops, SparseCore 0:
  35.9 82.1 all-gather.1
where the time goes:
time: 355 us; the launch traced here: 348 us
  waiting for transfers between devices  211 us (59%)
  local copies, waits for them, and re-layouts  56.5 us (16%)
  matrix products  23.9 us (7%)
  other arithmetic  23 us (6%)
  starting transfers between devices  17.7 us (5%)
  between operations  16.7 us (5%)
    all_to_all x1, waiting for transfers between devices, relay(): lax.all_to_all(lax.all_to_all(flattened, 'doc', split_axis=1, concat_axis...  120 us
    all_to_all x1, waiting for transfers between devices, relay(): lax.all_to_all(flattened, 'doc', split_axis=1, concat_axis=1, tiled=True)  88.5 us
    dot_general x2, matrix products, compute(): jnp.einsum('kgps,skd->kgpd', weights.astype(jnp.bfloat16), value_heads, p...  16.8 us
    unnamed x8, local copies, waits for them, and re-layouts  14.6 us
    all_to_all x1, local copies, waits for them, and re-layouts, relay(): lax.all_to_all(lax.all_to_all(flattened, 'doc', split_axis=1, concat_axis...  11.9 us
    slice x3, local copies, waits for them, and re-layouts, local(): summary_cache[1:]  11 us
    reduce_sum x2, other arithmetic, compute(): denominator = denominator * factor + jnp.sum(weights, axis=-1)  9.34 us
    all_to_all x1, starting transfers between devices, relay(): lax.all_to_all(lax.all_to_all(flattened, 'doc', split_axis=1, concat_axis...  7.18 us
  transfers between devices with their start and end apart: 4, of which 3 were waited for; matrix products, arithmetic and copies ran while one was open for 19% of the time, Pallas kernels for 0%

commit v1 on v0

v1 whole, which is shorter than its diff:
```python
import functools
import math

import jax
import jax.numpy as jnp
from jax import lax
from jax.experimental import pallas as pl
from jax.experimental.pallas import tpu as pltpu
from jax.sharding import PartitionSpec as P

QH = 32
KVH = 8
HD = 128
BLOCK = 128
SECTIONS = 2
GROUP = 4
SUMLEN = 256


NEGATIVE = -1e30


MESH = pl.DeviceIdType.MESH


def kernel(
    rows,
    ctx,
    cache,
    queries,
    counts,
    blocks,
    attended,
    relayed,
    kv,
    mid,
    q_vmem,
    out_vmem,
    bias,
    s1,
    r1_first,
    r1,
    up_sem,
    down_sem,
    side_sem,
    kv_sem,
    s2,
    r2,
    local_sem,
):
    layers, _, slots, feat = cache.shape
    own = queries.shape[0]
    pieces = slots // own
    chips = ctx // 2
    me = lax.axis_index("doc")
    c = lax.axis_index("ctx")
    z = c // 2
    core = c % 2
    def seen(chip):
        return ((2 * chip + 2) * own + slots - 1) // slots

    barrier = pltpu.get_barrier_semaphore()
    for k in range(1, rows):
        pl.semaphore_signal(barrier, inc=1, device_id=((me + k) % rows, c), device_id_type=MESH)
    for k in range(1, ctx):
        pl.semaphore_signal(barrier, inc=1, device_id=(me, (c + k) % ctx), device_id_type=MESH)

    own_kv = pltpu.make_async_copy(
        cache.at[0, me], kv.at[c, pl.ds(pl.multiple_of(me * slots, slots), slots)], local_sem.at[0]
    )
    own_kv.start()
    q_copy = pltpu.make_async_copy(queries, q_vmem, local_sem.at[1])
    own_mid = pltpu.make_async_copy(cache.at[pl.ds(1, layers - 1), me], mid.at[:, me], local_sem.at[2])
    pl.semaphore_wait(barrier, rows - 1 + ctx - 1)

    def doc(ref, slice_index, j):
        return ref.at[slice_index, pl.ds(pl.multiple_of(j * slots, slots), slots)]

    def first_copy(j_to, j_from):
        return pltpu.make_async_remote_copy(
            src_ref=cache.at[0, j_to],
            dst_ref=doc(kv, c, j_from),
            send_sem=s1,
            recv_sem=r1_first.at[j_from],
            device_id=(j_to, c),
            device_id_type=MESH,
        )

    for k in range(1, rows):
        first_copy((me + k) % rows, me).start()
    own_mid.start()
    q_copy.start()

    def row_copy(l, j_to):
        return pltpu.make_async_remote_copy(
            src_ref=cache.at[l, j_to],
            dst_ref=mid.at[l - 1, me],
            send_sem=s1,
            recv_sem=r1.at[l],
            device_id=(j_to, c),
            device_id_type=MESH,
        )

    @pl.loop(1, layers)
    def _(l):
        for k in range(1, rows):
            row_copy(l, (me + k) % rows).start()

    def kv_copy(slice_index, j, sems, target):
        return pltpu.make_async_remote_copy(
            src_ref=doc(kv, slice_index, j),
            dst_ref=doc(kv, slice_index, j),
            send_sem=sems.at[slice_index, j],
            recv_sem=kv_sem.at[slice_index, j],
            device_id=(me, target),
            device_id_type=MESH,
        )

    def pass_on(slice_index, j, upward, downward):
        if upward:

            @pl.when(z < chips - 1)
            def _():
                kv_copy(slice_index, j, up_sem, c + 2).start()

        if downward:

            @pl.when((z > 0) & (j < seen(z - 1)))
            def _():
                kv_copy(slice_index, j, down_sem, c - 2).start()

        @pl.when(j < seen(z))
        def _():
            kv_copy(slice_index, j, side_sem, c + 1 - 2 * core).start()

    def spread(l, chosen):
        for k in chosen:
            t = (c + k) % ctx
            j = t // pieces
            h = t % pieces
            pltpu.make_async_remote_copy(
                src_ref=mid.at[l - 1, j, pl.ds(pl.multiple_of(h * own, own), own)],
                dst_ref=relayed.at[l, :, pl.ds(pl.multiple_of(c * feat, feat), feat)],
                send_sem=s2,
                recv_sem=r2,
                device_id=(me, t),
                device_id_type=MESH,
            ).start()

    def layer_step(l):
        arrived = mid.at[l - 1, pl.ds(0, rows - 1)]
        pltpu.make_async_copy(arrived, arrived, r1.at[l]).wait()
        spread(l, range(1, ctx))
        pltpu.make_async_copy(
            mid.at[l - 1, c // pieces, pl.ds(pl.multiple_of((c % pieces) * own, own), own)],
            relayed.at[l, :, pl.ds(pl.multiple_of(c * feat, feat), feat)],
            local_sem.at[3],
        ).start()

    own_kv.wait()
    pass_on(c, me, True, True)
    for k in range(1, rows):
        j = (me + k) % rows
        first_copy(me, j).wait_recv()
        pass_on(c, j, True, True)
    own_mid.wait()
    for step in range(1, chips):

        @pl.when(z >= step)
        def _():
            for k in range(rows):
                j = (me + k) % rows
                kv_copy(c - 2 * step, j, up_sem, c).wait_recv()
                pass_on(c - 2 * step, j, True, False)

        @pl.when(z + step < chips)
        def _():
            for k in range(rows):
                j = (me + k) % rows

                @pl.when(j < seen(z))
                def _():
                    kv_copy(c + 2 * step, j, down_sem, c).wait_recv()
                    pass_on(c + 2 * step, j, False, True)

        layer_step(step)

    @pl.loop(0, seen(z))
    def _(j):
        at = j * rows + me
        key = lax.broadcasted_iota(jnp.int32, (own, slots), 1)
        query = lax.broadcasted_iota(jnp.int32, (own, slots), 0)
        section = key // SUMLEN
        reach = jnp.zeros((own, slots), jnp.int32)
        for s in range(SECTIONS):
            reach = jnp.where((section == s) & (s < counts[at]), BLOCK * blocks[at, s], reach)
        allowed = (key - section * SUMLEN < reach) & (j * slots + key <= c * own + query)
        bias[j] = jnp.where(allowed, 0.0, NEGATIVE)

    for other in range(chips):
        slice_index = 2 * other + 1 - core

        @pl.loop(0, seen(z))
        def _(j):
            kv_copy(slice_index, j, side_sem, c).wait_recv()

    q_copy.wait()
    for t in range(ctx):
        pltpu.make_async_copy(
            kv.at[t, pl.ds(pl.multiple_of(c * own, own), own)],
            relayed.at[0, :, pl.ds(t * feat, feat)],
            local_sem.at[4],
        ).start()

    factor = math.log2(math.e) / math.sqrt(HD)

    @pl.loop(0, KVH)
    def _(k):
        @pl.when(k + chips < layers)
        def _():
            layer_step(k + chips)

        per = feat // HD
        key_slice = k // per
        value_slice = (KVH + k) // per
        lanes = pl.ds(pl.multiple_of((k % per) * HD, HD), HD)
        for i in range(GROUP):
            column = pl.ds(pl.multiple_of((k * GROUP + i) * HD, HD), HD)
            q = q_vmem[:, column]

            def block(j, state):
                top, total, acc = state
                at = pl.ds(pl.multiple_of(j * slots, slots), slots)
                s = lax.dot_general(
                    q, kv[key_slice, at, lanes], (((1,), (1,)), ((), ())), preferred_element_type=jnp.float32
                )
                s = s + bias[j]
                newest = jnp.maximum(top, jnp.max(s, axis=1, keepdims=True))
                w = jnp.exp2((s - newest) * factor)
                shrink = jnp.exp2((top - newest) * factor)
                total = total * shrink + jnp.sum(w, axis=1, keepdims=True)
                acc = acc * shrink + jnp.dot(
                    w.astype(jnp.bfloat16), kv[value_slice, at, lanes], preferred_element_type=jnp.float32
                )
                return newest, total, acc

            start = (
                jnp.full((own, 1), NEGATIVE, jnp.float32),
                jnp.zeros((own, 1), jnp.float32),
                jnp.zeros((own, HD), jnp.float32),
            )
            _, total, acc = lax.fori_loop(0, seen(z), block, start)
            out_vmem[:, column] = (acc / total).astype(jnp.bfloat16)

    out_copy = pltpu.make_async_copy(out_vmem, attended, local_sem.at[1])
    out_copy.start()

    @pl.loop(0, ctx)
    def _(t):
        @pl.loop(0, rows)
        def _(j):
            @pl.when(t % 2 == core)
            def _():
                chip = t // 2

                @pl.when((z < chips - 1) & (chip <= z))
                def _():
                    kv_copy(t, j, up_sem, c).wait_send()

                @pl.when((z > 0) & (j < seen(z - 1)) & (chip >= z))
                def _():
                    kv_copy(t, j, down_sem, c).wait_send()

                @pl.when(j < seen(z))
                def _():
                    kv_copy(t, j, side_sem, c).wait_send()

    def sized(ref, sem):
        return pltpu.make_async_copy(ref, ref, sem)

    sized(cache.at[:, pl.ds(0, rows - 1)], s1).wait()
    passed = relayed.at[pl.ds(1, layers - 1), :, pl.ds(0, (ctx - 1) * feat)]
    sized(passed, s2).wait()
    sized(passed, r2).wait()
    sized(relayed.at[pl.ds(1, layers - 1), :, pl.ds(0, feat)], local_sem.at[3]).wait()
    sized(relayed.at[0], local_sem.at[4]).wait()
    out_copy.wait()


def local(summary_cache, queries, section_counts, summary_blocks):
    rows = lax.axis_size("doc")
    ctx = lax.axis_size("ctx")
    layers, documents, slots, feat = summary_cache.shape
    own = queries.shape[1]
    dtype = summary_cache.dtype
    any_space = pl.BlockSpec(memory_space=pl.ANY)
    scalars = pl.BlockSpec(memory_space=pltpu.SMEM)
    dma = pltpu.SemaphoreType.DMA
    attended, relayed = pl.pallas_call(
        functools.partial(kernel, rows, ctx),
        out_shape=(
            jax.ShapeDtypeStruct(queries.shape[1:], dtype),
            jax.ShapeDtypeStruct((layers, own, ctx * feat), dtype),
        ),
        in_specs=[any_space, any_space, scalars, scalars],
        out_specs=(any_space, any_space),
        scratch_shapes=[
            pltpu.VMEM((ctx, rows * slots, feat), dtype),
            pltpu.VMEM((layers - 1, rows, slots, feat), dtype),
            pltpu.VMEM(queries.shape[1:], dtype),
            pltpu.VMEM(queries.shape[1:], dtype),
            pltpu.VMEM((rows, own, slots), jnp.float32),
            dma,
            dma((rows,)),
            dma((layers,)),
            dma((ctx, rows)),
            dma((ctx, rows)),
            dma((ctx, rows)),
            dma((ctx, rows)),
            dma,
            dma,
            dma((5,)),
        ],
        compiler_params=pltpu.CompilerParams(
            collective_id=0, has_side_effects=True, vmem_limit_bytes=60 * 1024 * 1024
        ),
    )(summary_cache, queries[0], section_counts, summary_blocks)
    return attended[None], relayed[:, None]


def solution(mesh):
    placed = (P(None, "doc", None, "ctx"), P("doc", "ctx", None), P(), P())
    return jax.shard_map(
        local,
        mesh=mesh,
        in_specs=placed,
        out_specs=(P("doc", "ctx", None), P(None, "doc", "ctx", None)),
        check_vma=False,
    )
```

time: 355 us -> 234 us (0.66); the launches traced: 348 us -> 233 us
  Pallas kernels: 0 us -> 220 us
  waiting for transfers between devices: 211 us -> 0 us
  local copies, waits for them, and re-layouts: 56.5 us -> 12.9 us
  matrix products: 23.9 us -> 0 us
  other arithmetic: 23 us -> 0 us
  starting transfers between devices: 17.7 us -> 0 us
  between operations: 16.7 us -> 0.64 us
    pallas_call x0 -> x1, Pallas kernels: none -> 220 us  [local(): pl.pallas_call(functools.partial(kernel, rows, ctx), out_shape=(jax.Shape...]
    all_to_all x3 -> x0, waiting for transfers between devices: 211 us -> none  [the longest x1 120 us: relay(): lax.all_to_all(lax.all_to_all(flattened, 'doc', split_axis=1, concat_axis...]
    dot_general x4 -> x0, matrix products: 23.9 us -> none  [the longest x2 16.8 us: compute(): jnp.einsum('kgps,skd->kgpd', weights.astype(jnp.bfloat16), value_heads, p...]
    slice x7 -> x0, local copies, waits for them, and re-layouts: 18.9 us -> none  [the longest x3 11 us: local(): summary_cache[1:]]
    all_to_all x3 -> x0, starting transfers between devices: 17.7 us -> none  [the longest x1 7.18 us: relay(): lax.all_to_all(lax.all_to_all(flattened, 'doc', split_axis=1, concat_axis...]
    all_to_all x3 -> x0, local copies, waits for them, and re-layouts: 16.5 us -> none  [the longest x1 11.9 us: relay(): lax.all_to_all(lax.all_to_all(flattened, 'doc', split_axis=1, concat_axis...]
    reduce_sum x4 -> x0, other arithmetic: 9.6 us -> none  [the longest x2 9.34 us: compute(): denominator = denominator * factor + jnp.sum(weights, axis=-1)]
    reshape x1 -> x0, other arithmetic: 7.04 us -> none  [local(): relayed_local.reshape(relayed_local.shape[0], 1, own_rows, relayed_local....]
  transfers between devices with their start and end apart: 4 -> 0, of which waited for: 3 -> 0; matrix products, arithmetic and copies ran while one was open for 19% -> 0% of each run, Pallas kernels for 0% -> 0%
where the time goes in v1:
time: 234 us; the launch traced here: 233 us
  Pallas kernels  220 us (94%)
  local copies, waits for them, and re-layouts  12.9 us (6%)
    pallas_call x1, Pallas kernels, local(): pl.pallas_call(functools.partial(kernel, rows, ctx), out_shape=(jax.Shape...  220 us
    unnamed x3, local copies, waits for them, and re-layouts  12.9 us

profile of v1, /device:TPU:13, one launch (start us, length us, event | category | flops | bytes accessed | tf_op | source)
XLA Modules:
  0.0 233.3 jit_solution(12078424651289881726)
XLA Ops:
  0.6 1.4 copy.6.blocks
  2.0 219.7 %shard_map.59 = (bf16[256,4096]{1,0:T(8,128)(2,1)}, bf16[8,256,2048]{2,1,0:T(8,128)(2,1)}) custom-call(bf16[8,4,512,256]{3,2,1,0:T(8,128)(2,1)} %cache.1, bf16[256,4096]{1,0:T(8,128)(2,1)} %bitcast.7, s32[16]{0:T(128)} %counts.1, s32[16,2]{1,0:T(8,128)} %copy.6.blocks), custom_call_target="tpu_custom_call" | custom-call | tf_op jit(solution)/shard_map/pallas_call | solution.py:299
  221.7 3.1 %copy.10 = bf16[1,256,4096]{2,1,0:T(8,128)(2,1)} copy(bf16[1,256,4096]{2,1,0:T(8,128)(2,1)} %bitcast.6) | data formatting | bytes 4194304
  224.8 8.4 %copy.11 = bf16[8,1,256,2048]{3,2,1,0:T(8,128)(2,1)} copy(bf16[8,1,256,2048]{3,2,1,0:T(8,128)(2,1)} %bitcast.5) | data formatting | bytes 16777216

commit v2 on v1

--- a/solution.py
+++ b/solution.py
@@ -56,12 +56,22 @@
     c = lax.axis_index("ctx")
     z = c // 2
     core = c % 2
+    def partner(k):
+        if rows & (rows - 1):
+            return (me + k) % rows
+        row, bit = me, 1
+        while bit < rows:
+            if k & bit:
+                row = row + bit * (1 - 2 * ((me // bit) % 2))
+            bit *= 2
+        return row
+
     def seen(chip):
         return ((2 * chip + 2) * own + slots - 1) // slots
 
     barrier = pltpu.get_barrier_semaphore()
     for k in range(1, rows):
-        pl.semaphore_signal(barrier, inc=1, device_id=((me + k) % rows, c), device_id_type=MESH)
+        pl.semaphore_signal(barrier, inc=1, device_id=(partner(k), c), device_id_type=MESH)
     for k in range(1, ctx):
         pl.semaphore_signal(barrier, inc=1, device_id=(me, (c + k) % ctx), device_id_type=MESH)
 
@@ -87,7 +97,7 @@
         )
 
     for k in range(1, rows):
-        first_copy((me + k) % rows, me).start()
+        first_copy(partner(k), me).start()
     own_mid.start()
     q_copy.start()
 
@@ -104,7 +114,7 @@
     @pl.loop(1, layers)
     def _(l):
         for k in range(1, rows):
-            row_copy(l, (me + k) % rows).start()
+            row_copy(l, partner(k)).start()
 
     def kv_copy(slice_index, j, sems, target):
         return pltpu.make_async_remote_copy(
@@ -133,57 +143,76 @@
         def _():
             kv_copy(slice_index, j, side_sem, c + 1 - 2 * core).start()
 
-    def spread(l, chosen):
-        for k in chosen:
-            t = (c + k) % ctx
-            j = t // pieces
-            h = t % pieces
-            pltpu.make_async_remote_copy(
-                src_ref=mid.at[l - 1, j, pl.ds(pl.multiple_of(h * own, own), own)],
-                dst_ref=relayed.at[l, :, pl.ds(pl.multiple_of(c * feat, feat), feat)],
-                send_sem=s2,
-                recv_sem=r2,
-                device_id=(me, t),
-                device_id_type=MESH,
+    def send_piece(l, t):
+        j = t // pieces
+        h = t % pieces
+        pltpu.make_async_remote_copy(
+            src_ref=mid.at[l - 1, j, pl.ds(pl.multiple_of(h * own, own), own)],
+            dst_ref=relayed.at[l, :, pl.ds(pl.multiple_of(c * feat, feat), feat)],
+            send_sem=s2,
+            recv_sem=r2,
+            device_id=(me, t),
+            device_id_type=MESH,
+        ).start()
+
+    def spread(l, distances):
+        for d in distances:
+            for other in (core, 1 - core):
+
+                @pl.when(z + d < chips)
+                def _():
+                    send_piece(l, 2 * (z + d) + other)
+
+                @pl.when(z >= d)
+                def _():
+                    send_piece(l, 2 * (z - d) + other)
+
+    def layer_step(l):
+        if l < layers:
+            arrived = mid.at[l - 1, pl.ds(0, rows - 1)]
+            pltpu.make_async_copy(arrived, arrived, r1.at[l]).wait()
+        for d in range(1, chips):
+            late = l - (d - 1)
+            if 0 < late < layers:
+                spread(late, [d])
+        if l < layers:
+            send_piece(l, c + 1 - 2 * core)
+            pltpu.make_async_copy(
+                mid.at[l - 1, c // pieces, pl.ds(pl.multiple_of((c % pieces) * own, own), own)],
+                relayed.at[l, :, pl.ds(pl.multiple_of(c * feat, feat), feat)],
+                local_sem.at[3],
             ).start()
-
-    def layer_step(l):
-        arrived = mid.at[l - 1, pl.ds(0, rows - 1)]
-        pltpu.make_async_copy(arrived, arrived, r1.at[l]).wait()
-        spread(l, range(1, ctx))
-        pltpu.make_async_copy(
-            mid.at[l - 1, c // pieces, pl.ds(pl.multiple_of((c % pieces) * own, own), own)],
-            relayed.at[l, :, pl.ds(pl.multiple_of(c * feat, feat), feat)],
-            local_sem.at[3],
-        ).start()
 
     own_kv.wait()
     pass_on(c, me, True, True)
     for k in range(1, rows):
-        j = (me + k) % rows
+        j = partner(k)
         first_copy(me, j).wait_recv()
         pass_on(c, j, True, True)
     own_mid.wait()
+    next_step = 1
     for step in range(1, chips):
 
         @pl.when(z >= step)
         def _():
             for k in range(rows):
-                j = (me + k) % rows
+                j = partner(k)
                 kv_copy(c - 2 * step, j, up_sem, c).wait_recv()
                 pass_on(c - 2 * step, j, True, False)
 
         @pl.when(z + step < chips)
         def _():
             for k in range(rows):
-                j = (me + k) % rows
+                j = partner(k)
 
                 @pl.when(j < seen(z))
                 def _():
                     kv_copy(c + 2 * step, j, down_sem, c).wait_recv()
                     pass_on(c + 2 * step, j, False, True)
 
-        layer_step(step)
+        for _ in range(2):
+            layer_step(next_step)
+            next_step += 1
 
     @pl.loop(0, seen(z))
     def _(j):
@@ -193,7 +222,7 @@
         section = key // SUMLEN
         reach = jnp.zeros((own, slots), jnp.int32)
         for s in range(SECTIONS):
-            reach = jnp.where((section == s) & (s < counts[at]), BLOCK * blocks[at, s], reach)
+            reach = jnp.where((section == s) & (s < counts[at]), BLOCK * blocks[s, at], reach)
         allowed = (key - section * SUMLEN < reach) & (j * slots + key <= c * own + query)
         bias[j] = jnp.where(allowed, 0.0, NEGATIVE)
 
@@ -214,11 +243,15 @@
 
     factor = math.log2(math.e) / math.sqrt(HD)
 
+    last_step = layers + chips - 2
+
     @pl.loop(0, KVH)
     def _(k):
-        @pl.when(k + chips < layers)
-        def _():
-            layer_step(k + chips)
+        for l in range(next_step, last_step):
+
+            @pl.when(k == l - next_step)
+            def _():
+                layer_step(l)
 
         per = feat // HD
         key_slice = k // per
@@ -287,6 +320,31 @@
     out_copy.wait()
 
 
+def copy_out(attended, relayed, attended_out, relayed_out, sems):
+    layers = relayed.shape[0]
+    copies = [pltpu.make_async_copy(relayed.at[l], relayed_out.at[l], sems.at[l]) for l in range(layers)]
+    copies.append(pltpu.make_async_copy(attended, attended_out, sems.at[layers]))
+    for copy in copies:
+        copy.start()
+    for copy in copies:
+        copy.wait()
+
+
+def deliver(attended, relayed):
+    any_space = pl.BlockSpec(memory_space=pl.ANY)
+    return pl.pallas_call(
+        copy_out,
+        out_shape=(
+            jax.ShapeDtypeStruct(attended.shape, attended.dtype),
+            jax.ShapeDtypeStruct(relayed.shape, relayed.dtype),
+        ),
+        in_specs=[any_space, any_space],
+        out_specs=(any_space, any_space),
+        scratch_shapes=[pltpu.SemaphoreType.DMA((relayed.shape[0] + 1,))],
+        compiler_params=pltpu.CompilerParams(vmem_limit_bytes=4 * 1024 * 1024),
+    )(attended, relayed)
+
+
 def local(summary_cache, queries, section_counts, summary_blocks):
     rows = lax.axis_size("doc")
     ctx = lax.axis_size("ctx")
@@ -294,15 +352,23 @@
     own = queries.shape[1]
     dtype = summary_cache.dtype
     any_space = pl.BlockSpec(memory_space=pl.ANY)
+    held = pl.BlockSpec(memory_space=pltpu.HBM)
     scalars = pl.BlockSpec(memory_space=pltpu.SMEM)
     dma = pltpu.SemaphoreType.DMA
+    size = rows * slots * feat * (ctx + layers - 1) * 2 + own * queries.shape[2] * 4 + rows * own * slots * 4
+    room = size + own * (layers * ctx * feat + queries.shape[2]) * 2 + 4 * 1024 * 1024
+    place = pltpu.VMEM if room < 60 * 1024 * 1024 else pltpu.HBM
+
+    def in_hbm(array):
+        return pltpu.with_memory_space_constraint(array, pltpu.HBM)
+
     attended, relayed = pl.pallas_call(
         functools.partial(kernel, rows, ctx),
         out_shape=(
-            jax.ShapeDtypeStruct(queries.shape[1:], dtype),
-            jax.ShapeDtypeStruct((layers, own, ctx * feat), dtype),
+            place(queries.shape[1:], dtype),
+            place((layers, own, ctx * feat), dtype),
         ),
-        in_specs=[any_space, any_space, scalars, scalars],
+        in_specs=[held, held, scalars, scalars],
         out_specs=(any_space, any_space),
         scratch_shapes=[
             pltpu.VMEM((ctx, rows * slots, feat), dtype),
@@ -322,10 +388,10 @@
             dma((5,)),
         ],
         compiler_params=pltpu.CompilerParams(
-            collective_id=0, has_side_effects=True, vmem_limit_bytes=60 * 1024 * 1024
+            collective_id=0, has_side_effects=True, vmem_limit_bytes=size + 3 * 1024 * 1024
         ),
-    )(summary_cache, queries[0], section_counts, summary_blocks)
-    return attended[None], relayed[:, None]
+    )(*(in_hbm(x) for x in (summary_cache, queries[0], section_counts, summary_blocks.T)))
+    return deliver(attended[None], relayed[:, None])
 
 
 def solution(mesh):

time: 234 us -> 215 us (0.919)
  local copies, waits for them, and re-layouts: 12.9 us -> 0 us
  Pallas kernels: 220 us -> 212 us
    unnamed x3 -> x0, local copies, waits for them, and re-layouts: 12.9 us -> none
    pallas_call x1 -> x2, Pallas kernels: 220 us -> 212 us  [the longest x1 208 us: local(): pl.pallas_call(functools.partial(kernel, rows, ctx), out_shape=(place(que...]
where the time goes in v2:
time: 215 us; the launch traced here: 213 us
  Pallas kernels  212 us (99%)
    pallas_call x1, Pallas kernels, local(): pl.pallas_call(functools.partial(kernel, rows, ctx), out_shape=(place(que...  208 us

profile of v2, /device:TPU:13, one launch (start us, length us, event | category | flops | bytes accessed | tf_op | source)
XLA Modules:
  0.0 213.0 jit_solution(15254556943648564575)
XLA Ops:
  0.6 208.3 %shard_map.59 = (bf16[256,4096]{1,0:T(8,128)(2,1)S(1)}, bf16[8,256,2048]{2,1,0:T(8,128)(2,1)S(1)}) custom-call(bf16[8,4,512,256]{3,2,1,0:T(8,128)(2,1)} %cache.1, bf16[256,4096]{1,0:T(8,128)(2,1)} %bitcast.6, s32[16]{0:T(128)} %counts.1, s32[2,16]{1,0:T(2,128)} %bitcast.7), custom_call_target="tpu_custom_call" | custom-call | tf_op jit(solution)/shard_map/pallas_call | solution.py:365
  209.0 4.0 %shard_map.60 = (bf16[1,256,4096]{2,1,0:T(8,128)(2,1)}, bf16[8,1,256,2048]{3,2,1,0:T(8,128)(2,1)}) custom-call(bf16[1,256,4096]{2,1,0:T(8,128)(2,1)S(1)} %bitcast.5, bf16[8,1,256,2048]{3,2,1,0:T(8,128)(2,1)S(1)} %bitcast.4), custom_call_target="tpu_custom_call" | custom-call | tf_op jit(solution)/shard_map/pallas_call | solution.py:335
